TPU v7x, 32 devices: a whole 2x2x4 slice. The times are simulated.
32 devices in a mesh: wide: 16 (over z, y, core), narrow: 2 (over x).
Axes of the slice: x: 2, y: 2, z: 4, core: 2. Of those that a mesh axis runs over, the one named last changes fastest.
Arguments:
- hidden_in: bfloat16 [16384, 1024], P(('wide', 'narrow')), may hold values from -6 to 6
- segment_ids: int32 [32, 512], P(('wide', 'narrow')), may hold values from 0 to 7, never falling along the last dimension, each value on 1 to 256 neighbouring positions
- expert_ids: int32 [16384, 8], P(('wide', 'narrow')), may hold values from 0 to 15, all different within a row; in each aligned block of 512 rows (0 to 511, 512 to 1023, ...) at most 512 rows name the same one
- attn_gain: float32 [1024], replicated, may hold values from 0.5 to 1.5
- w_query: bfloat16 [1024, 1024], replicated, may hold values from -0.1875 to 0.1875
- w_key: bfloat16 [1024, 512], replicated, may hold values from -0.1875 to 0.1875
- w_value: bfloat16 [1024, 512], replicated, may hold values from -0.1875 to 0.1875
- w_out: bfloat16 [1024, 1024], replicated, may hold values from -0.75 to 0.75
- ffn_gain: float32 [1024], replicated, may hold values from 0.5 to 1.5
- router: bfloat16 [1024, 16], replicated, may hold values from -0.1875 to 0.1875
- w_gate: bfloat16 [16, 1024, 512], P('wide', None, 'narrow'), may hold values from -0.1875 to 0.1875
- w_up: bfloat16 [16, 1024, 512], P('wide', None, 'narrow'), may hold values from -0.1875 to 0.1875
- w_down: bfloat16 [16, 512, 1024], P('wide', 'narrow'), may hold values from -0.75 to 0.75
- grad_out: bfloat16 [16384, 1024], P(('wide', 'narrow')), may hold values from -6 to 6
Outputs:
- hidden_out: bfloat16 [16384, 1024], P(('wide', 'narrow'))
- grad_in: bfloat16 [16384, 1024], P(('wide', 'narrow'))
- grad_attn_gain: float32 [1024], replicated
- grad_query: float32 [1024, 1024], replicated
- grad_key: float32 [1024, 512], replicated
- grad_value: float32 [1024, 512], replicated
- grad_out_proj: float32 [1024, 1024], replicated
- grad_ffn_gain: float32 [1024], replicated
- grad_router: float32 [1024, 16], replicated
- grad_gate: float32 [16, 1024, 512], P('wide', None, 'narrow')
- grad_up: float32 [16, 1024, 512], P('wide', None, 'narrow')
- grad_down: float32 [16, 512, 1024], P('wide', 'narrow')
Inputs may be any that keep to these rules, and one draw needn't show every extreme that they name: `segment_ids`: each packed row has 8 documents numbered in order from 0, each of 1 to half of 512 tokens, one of exactly half of 512. `expert_ids`: each token names 8 different experts. Among the 512 tokens of one packed row no expert is named more than 512 times, and in every draw some row names some expert exactly 512 times.
All inputs are finite; a program needn't handle non-finite values.
Results may differ from a plain program's by a relative error of at most 0.015.
Values may be sent and summed in bfloat16 or wider, within the bound.
A program may use at most 320 MiB of HBM per device.

v0:
```python
import jax
import jax.numpy as jnp
from jax import lax
from jax.sharding import PartitionSpec as P

HD = 64
EPSILON = 1e-05


def norm_scale(values):
    return lax.rsqrt(jnp.mean(values * values, axis=-1, keepdims=True) + EPSILON)


def norm_back(values, inv_rms, gain_vector, grad_rows):
    weighted = grad_rows * gain_vector
    inner = jnp.mean(weighted * values, axis=-1, keepdims=True)
    value_grad = inv_rms * weighted - values * (inv_rms * inv_rms * inv_rms) * inner
    return (value_grad, jnp.sum(grad_rows * values * inv_rms, axis=0))


def rope_tables(length, head_dim):
    half_size = head_dim // 2
    freqs = 10000.0 ** (-(jnp.arange(half_size, dtype=jnp.float32) * 2.0) / head_dim)
    angles = jnp.arange(length, dtype=jnp.float32)[:, None] * freqs[None, :]
    return (jnp.cos(angles), jnp.sin(angles))


def rotate(values, cosine_table, sine_table, direction):
    half_size = values.shape[-1] // 2
    first_half = values[..., :half_size]
    second_half = values[..., half_size:]
    cosine_part = cosine_table[:, None, :]
    sine_part = sine_table[:, None, :] * direction
    return jnp.concatenate(
        [
            first_half * cosine_part - second_half * sine_part,
            second_half * cosine_part + first_half * sine_part,
        ],
        axis=-1,
    )


def attention_probs(grouped, key_rows, allowed, head_dim):
    scores = jnp.einsum(
        "qngd,knd->ngqk", grouped, key_rows, preferred_element_type=jnp.float32
    ) * head_dim ** (-0.5)
    return jnp.where(allowed, scores, -1e30)


def on_device(
    hidden_in,
    segment_ids,
    expert_ids,
    attn_gain,
    w_query,
    w_key,
    w_value,
    w_out,
    ffn_gain,
    router,
    w_gate,
    w_up,
    w_down,
    grad_out,
):
    f32 = jnp.float32
    bf16 = jnp.bfloat16
    length, model_width = hidden_in.shape
    head_dim = HD
    head_count = w_query.shape[1] // head_dim
    kv_count = w_key.shape[1] // head_dim
    group_size = head_count // kv_count
    experts = router.shape[1]
    rows_grad = lax.all_gather(grad_out, "wide", axis=0, tiled=True)
    full_gate, full_up, full_down = (
        lax.all_gather(w_gate, "narrow", axis=2, tiled=True),
        lax.all_gather(w_up, "narrow", axis=2, tiled=True),
        lax.all_gather(w_down, "narrow", axis=1, tiled=True),
    )
    inputs = hidden_in.astype(f32)
    scale_one = norm_scale(inputs)
    normed = (inputs * scale_one * attn_gain).astype(bf16)
    query_pre = jnp.dot(normed, w_query, preferred_element_type=f32)
    key_pre = jnp.dot(normed, w_key, preferred_element_type=f32)
    value_pre = jnp.dot(normed, w_value, preferred_element_type=f32)
    cosine_table, sine_table = rope_tables(length, head_dim)
    query_rows = rotate(
        query_pre.reshape(length, head_count, head_dim), cosine_table, sine_table, 1.0
    ).astype(bf16)
    key_rows = rotate(
        key_pre.reshape(length, kv_count, head_dim), cosine_table, sine_table, 1.0
    ).astype(bf16)
    value_rows = value_pre.astype(bf16).reshape(length, kv_count, head_dim)
    grouped = query_rows.reshape(length, kv_count, group_size, head_dim)
    segments = segment_ids[0]
    places = jnp.arange(length, dtype=jnp.int32)
    allowed = (segments[:, None] == segments[None, :]) & (places[:, None] >= places[None, :])
    scores = attention_probs(grouped, key_rows, allowed, head_dim)
    row_max = jnp.max(scores, axis=-1, keepdims=True)
    log_total = row_max + jnp.log(jnp.sum(jnp.exp(scores - row_max), axis=-1, keepdims=True))
    weights_prob = jnp.exp(scores - log_total)
    attended = jnp.einsum(
        "ngqk,knd->qngd", weights_prob.astype(bf16), value_rows, preferred_element_type=f32
    )
    attended = attended.reshape(length, head_count * head_dim).astype(bf16)
    mixed_rows = inputs + jnp.dot(attended, w_out, preferred_element_type=f32)
    scale_two = norm_scale(mixed_rows)
    ffn_normed = (mixed_rows * scale_two * ffn_gain).astype(bf16)
    logits = jnp.dot(ffn_normed, router, preferred_element_type=f32)
    picked = expert_ids[:, :, None] == jnp.arange(experts, dtype=jnp.int32)[None, None, :]
    member = jnp.any(picked, axis=1)
    masked = jnp.where(member, logits, -jnp.inf)
    powers = jnp.where(member, jnp.exp(masked - jnp.max(masked, axis=-1, keepdims=True)), 0.0)
    gate_probs = powers / jnp.sum(powers, axis=-1, keepdims=True)
    row_gates = lax.all_to_all(gate_probs.T, "wide", split_axis=0, concat_axis=0, tiled=True)
    row_gates = row_gates.reshape(-1, 1)
    rows_in = lax.all_gather(ffn_normed, "wide", axis=0, tiled=True)
    gate_act = jnp.dot(rows_in, full_gate[0], preferred_element_type=f32)
    up_act = jnp.dot(rows_in, full_up[0], preferred_element_type=f32)
    hidden_act = (jax.nn.silu(gate_act) * up_act).astype(bf16)
    outputs = jnp.dot(hidden_act, full_down[0], preferred_element_type=f32).astype(bf16)
    moe_rows = lax.psum_scatter(
        (row_gates * outputs.astype(f32)).astype(bf16), "wide", scatter_dimension=0, tiled=True
    )
    hidden_out = (mixed_rows + moe_rows.astype(f32)).astype(bf16)
    cotangent = grad_out.astype(f32)
    gate_dots = jnp.sum(outputs.astype(f32) * rows_grad.astype(f32), axis=-1)
    gate_grads = lax.all_to_all(
        gate_dots.reshape(experts, length), "wide", split_axis=0, concat_axis=0, tiled=True
    ).T
    logit_grads = (
        gate_probs * (gate_grads - jnp.sum(gate_probs * gate_grads, axis=-1, keepdims=True))
    ).astype(bf16)
    router_grad = jnp.einsum("sd,se->de", ffn_normed, logit_grads, preferred_element_type=f32)
    normed_two_grad = jnp.einsum("se,de->sd", logit_grads, router, preferred_element_type=f32)
    grads_in = (row_gates * rows_grad.astype(f32)).astype(bf16)
    hidden_grad = jnp.einsum("rd,fd->rf", grads_in, full_down[0], preferred_element_type=f32)
    down_w_grad = jnp.einsum("rf,rd->fd", hidden_act, grads_in, preferred_element_type=f32)
    sigmoid_gate = jax.nn.sigmoid(gate_act)
    gate_grad = (
        hidden_grad * up_act * sigmoid_gate * (1.0 + gate_act * (1.0 - sigmoid_gate))
    ).astype(bf16)
    up_grad = (hidden_grad * gate_act * sigmoid_gate).astype(bf16)
    gate_w_grad = jnp.einsum("rd,rf->df", rows_in, gate_grad, preferred_element_type=f32)
    up_w_grad = jnp.einsum("rd,rf->df", rows_in, up_grad, preferred_element_type=f32)
    copy_grads = (
        jnp.einsum("rf,df->rd", gate_grad, full_gate[0], preferred_element_type=f32)
        + jnp.einsum("rf,df->rd", up_grad, full_up[0], preferred_element_type=f32)
    ).astype(bf16)
    rows_back = lax.psum_scatter(copy_grads, "wide", scatter_dimension=0, tiled=True)
    gate_w_grad, up_w_grad, down_w_grad = (
        lax.psum_scatter(
            gate_w_grad[None].astype(jnp.bfloat16), "narrow", scatter_dimension=2, tiled=True
        ).astype(jnp.float32),
        lax.psum_scatter(
            up_w_grad[None].astype(jnp.bfloat16), "narrow", scatter_dimension=2, tiled=True
        ).astype(jnp.float32),
        lax.psum_scatter(
            down_w_grad[None].astype(jnp.bfloat16), "narrow", scatter_dimension=1, tiled=True
        ).astype(jnp.float32),
    )
    normed_two_grad = normed_two_grad + rows_back.astype(f32)
    mixed_part, ffn_gain_grad = norm_back(mixed_rows, scale_two, ffn_gain, normed_two_grad)
    mixed_grad = cotangent + mixed_part
    branch_grad = mixed_grad.astype(bf16)
    out_w_grad = jnp.einsum("sh,sd->hd", attended, branch_grad, preferred_element_type=f32)
    attended_grad = jnp.einsum("sd,hd->sh", branch_grad, w_out, preferred_element_type=f32).astype(
        bf16
    )
    attended_grad = attended_grad.reshape(length, kv_count, group_size, head_dim)
    scores = attention_probs(grouped, key_rows, allowed, head_dim)
    weights_prob = jnp.exp(scores - log_total)
    value_grad = jnp.einsum(
        "ngqk,qngd->knd", weights_prob.astype(bf16), attended_grad, preferred_element_type=f32
    )
    prob_grad = jnp.einsum("qngd,knd->ngqk", attended_grad, value_rows, preferred_element_type=f32)
    score_grad = (
        weights_prob * (prob_grad - jnp.sum(weights_prob * prob_grad, axis=-1, keepdims=True))
    ).astype(bf16)
    query_grad = jnp.einsum(
        "ngqk,knd->qngd", score_grad, key_rows, preferred_element_type=f32
    ) * head_dim ** (-0.5)
    key_grad = jnp.einsum(
        "ngqk,qngd->knd", score_grad, grouped, preferred_element_type=f32
    ) * head_dim ** (-0.5)
    query_grad = rotate(
        query_grad.reshape(length, head_count, head_dim), cosine_table, sine_table, -1.0
    )
    query_grad = query_grad.reshape(length, -1).astype(bf16)
    key_grad = rotate(key_grad, cosine_table, sine_table, -1.0).reshape(length, -1).astype(bf16)
    value_grad = value_grad.reshape(length, -1).astype(bf16)
    query_w_grad = jnp.einsum("sd,sh->dh", normed, query_grad, preferred_element_type=f32)
    key_w_grad = jnp.einsum("sd,sh->dh", normed, key_grad, preferred_element_type=f32)
    value_w_grad = jnp.einsum("sd,sh->dh", normed, value_grad, preferred_element_type=f32)
    normed_one_grad = (
        jnp.einsum("sh,dh->sd", query_grad, w_query, preferred_element_type=f32)
        + jnp.einsum("sh,dh->sd", key_grad, w_key, preferred_element_type=f32)
        + jnp.einsum("sh,dh->sd", value_grad, w_value, preferred_element_type=f32)
    )
    input_part, attn_gain_grad = norm_back(inputs, scale_one, attn_gain, normed_one_grad)
    grad_in = (mixed_grad + input_part).astype(bf16)
    small = jnp.concatenate(
        [
            attn_gain_grad.reshape(-1, 128),
            ffn_gain_grad.reshape(-1, 128),
            router_grad.reshape(-1, 128),
        ],
        axis=0,
    )
    everywhere = ("wide", "narrow")
    columns = jnp.concatenate([query_w_grad, key_w_grad, value_w_grad, out_w_grad], axis=1)
    shares = lax.psum_scatter(columns.astype(bf16), everywhere, scatter_dimension=0, tiled=True)
    columns = lax.all_gather(shares, everywhere, axis=0, tiled=True).astype(f32)
    small = lax.psum(small, everywhere)
    gain_rows = model_width // 128
    query_width, key_width = (w_query.shape[1], w_key.shape[1])
    summed = (
        small[:gain_rows].reshape(-1),
        columns[:, :query_width],
        columns[:, query_width : query_width + key_width],
        columns[:, query_width + key_width : query_width + 2 * key_width],
        columns[:, query_width + 2 * key_width :],
        small[gain_rows : 2 * gain_rows].reshape(-1),
        small[2 * gain_rows :].reshape(router.shape),
    )
    return (
        hidden_out,
        grad_in,
        summed[0],
        summed[1],
        summed[2],
        summed[3],
        summed[4],
        summed[5],
        summed[6],
        gate_w_grad,
        up_w_grad,
        down_w_grad,
    )


def solution(mesh):
    return jax.shard_map(
        on_device,
        mesh=mesh,
        in_specs=(
            P(("wide", "narrow"), None),
            P(("wide", "narrow"), None),
            P(("wide", "narrow"), None),
            P(),
            P(),
            P(),
            P(),
            P(),
            P(),
            P(),
            P("wide", None, "narrow"),
            P("wide", None, "narrow"),
            P("wide", "narrow", None),
            P(("wide", "narrow"), None),
        ),
        out_specs=(
            P(("wide", "narrow"), None),
            P(("wide", "narrow"), None),
            P(),
            P(),
            P(),
            P(),
            P(),
            P(),
            P(),
            P("wide", None, "narrow"),
            P("wide", None, "narrow"),
            P("wide", "narrow", None),
        ),
        check_vma=False,
    )
```

profile of v0, /device:TPU:0, one launch (start us, length us, event | category | flops | bytes accessed | tf_op | source)
XLA Modules:
  0.0 1261.6 jit_solution(9160530426510023094)
XLA Ops:
  58.9 116.9 %all-gather.7.cloned.1.call-done = bf16[8192,1024]{1,0:T(8,128)(2,1)} async-done(((bf16[512,1024]{1,0:T(8,128)(2,1)}), bf16[8192,1024]{1,0:T(8,128)(2,1)}) %all-gather.7.cloned.1.call-update) | async-done | bytes 16777232 | tf_op jit(solution)/shard_map/all_gather | solution.py:117
  175.9 16.5 %fusion.47 = f32[8192,512]{1,0:T(8,128)} fusion(bf16[8192,1024]{1,0:T(8,128)(2,1)} %all-gather.7.cloned.1.call-done, bf16[1,1024,512]{2,1,0:T(8,128)(2,1)} %all-gather.11.cloned.1.call-done), kind=kOutput, calls=%fused_computation.74 | convolution fusion | flops 8589934592 | bytes 34603008 | tf_op jit(solution)/shard_map/dot_general | solution.py:119
  196.9 16.0 %fusion.51 = f32[8192,512]{1,0:T(8,128)} fusion(bf16[8192,1024]{1,0:T(8,128)(2,1)} %all-gather.7.cloned.1.call-done, bf16[1,1024,512]{2,1,0:T(8,128)(2,1)} %all-gather.9.cloned.1.call-done), kind=kOutput, calls=%fused_computation.78 | convolution fusion | flops 8589934592 | bytes 34603008 | tf_op jit(solution)/shard_map/dot_general | solution.py:118
  219.6 128.5 %all-gather.15.cloned.1.call-done = bf16[8192,1024]{1,0:T(8,128)(2,1)} async-done(((bf16[512,1024]{1,0:T(8,128)(2,1)}), bf16[8192,1024]{1,0:T(8,128)(2,1)}) %all-gather.15.cloned.1.call-update) | async-done | bytes 16777232 | tf_op jit(solution)/shard_map/all_gather | solution.py:74
  348.1 32.2 %multiply_convert_fusion = (bf16[8192,512]{1,0:T(8,128)(2,1)}, bf16[8192,512]{1,0:T(8,128)(2,1)}, bf16[8192,512]{1,0:T(8,128)(2,1)}) fusion(f32[8192,512]{1,0:T(8,128)} %fusion.51, f32[8192,512]{1,0:T(8,128)} %fusion.47, bf16[1,512,1024]{2,1,0:T(8,128)(2,1)} %all-gather.13.cloned.1.call-done, bf16[8192,1024]{1,0:T(8,128)(2,1)} %all-gather.15.cloned.1.call-done, ...), kind=kOutput, calls=%fused_computation.13 | convolution fusion | flops 8682209280 | bytes 76578816 | tf_op jit(solution)/shard_map/rd,fd->rf/dot_general | solution.py:137
  380.3 18.8 %fusion.49 = f32[8192,1024]{1,0:T(8,128)} fusion(bf16[8192,512]{1,0:T(8,128)(2,1)} %get-tuple-element.65, bf16[1,1024,512]{2,1,0:T(8,128)(2,1)S(1)} %copy-done.62), kind=kOutput, calls=%fused_computation.76 | convolution fusion | flops 8589934592 | bytes 42991616 | tf_op jit(solution)/shard_map/rf,df->rd/dot_general | solution.py:147
  399.1 21.5 %add_convert_fusion = bf16[8192,1024]{1,0:T(8,128)(2,1)} fusion(f32[8192,1024]{1,0:T(8,128)} %fusion.49, bf16[8192,512]{1,0:T(8,128)(2,1)} %get-tuple-element.64, bf16[1,1024,512]{2,1,0:T(8,128)(2,1)S(1)} %copy-done.60), kind=kOutput, calls=%fused_computation.6 | convolution fusion | flops 8606711808 | bytes 59768832 | tf_op jit(solution)/shard_map/rf,df->rd/dot_general | solution.py:148
  421.9 23.7 %fusion.1 = (f32[8192]{0:T(1024)S(1)}, bf16[8192,1024]{1,0:T(8,128)(2,1)}) fusion(bf16[8192,1024]{1,0:T(8,128)(2,1)} %all-gather.15.cloned.1.call-done, f32[8192]{0:T(1024)S(1)} %bitcast.185, bf16[8192,512]{1,0:T(8,128)(2,1)} %get-tuple-element.66, bf16[1,512,1024]{2,1,0:T(8,128)(2,1)S(1)} %copy-done.61), kind=kOutput, calls=%fused_computation.4 | convolution fusion | flops 8648646656 | bytes 43057152 | tf_op jit(solution)/shard_map/dot_general | solution.py:121
  445.7 9.3 all_to_all.21
  455.1 141.1 %reduce-scatter.11.cloned.1.call-done = bf16[512,1024]{1,0:T(8,128)(2,1)} async-done(((bf16[8192,1024]{1,0:T(8,128)(2,1)}), bf16[512,1024]{1,0:T(8,128)(2,1)}) %reduce-scatter.11.cloned.1.call-update) | async-done | bytes 1048592 | tf_op jit(solution)/shard_map/reduce_scatter | solution.py:150
  600.2 176.6 %reduce-scatter.9.cloned.1.call-done = bf16[512,1024]{1,0:T(8,128)(2,1)} async-done(((bf16[8192,1024]{1,0:T(8,128)(2,1)}), bf16[512,1024]{1,0:T(8,128)(2,1)}) %reduce-scatter.9.cloned.1.call-update) | async-done | bytes 1048592 | tf_op jit(solution)/shard_map/reduce_scatter | solution.py:122
  788.5 9.4 fusion.41
  797.9 16.0 %fusion.3 = (f32[8,2,512]{2,1,0:T(2,128)}, f32[8,512,512,2]{2,1,3,0:T(8,128)}) fusion(f32[8,2,512,512]{2,3,1,0:T(8,128)} %get-tuple-element.93, f32[8,2,512]{2,1,0:T(2,128)S(1)} %bitcast.181, bf16[512,8,64,1]{0,2,3,1:T(8,128)(2,1)} %bitcast.165, bf16[512,8,2,64]{0,3,2,1:T(8,128)(2,1)} %bitcast.160), kind=kOutput, calls=%fused_computation.9 | convolution fusion | flops 549445632 | bytes 35192832 | tf_op jit(solution)/shard_map/qngd,knd->ngqk/dot_general | solution.py:176
  814.0 11.1 fusion.5
  838.8 15.2 %pad_maximum_fusion = bf16[1024,3072]{0,1:T(8,128)(2,1)} fusion(bf16[1024,1024]{0,1:T(8,128)(2,1)S(1)} %copy-done.20, bf16[1024,512]{0,1:T(8,128)(2,1)S(1)} %convolution_convert_fusion.6, bf16[1024,512]{0,1:T(8,128)(2,1)S(1)} %convolution_convert_fusion.7, bf16[1024,1024]{0,1:T(8,128)(2,1)S(1)} %convolution_convert_fusion.1), kind=kLoop, calls=%fused_computation.23 | loop fusion | flops 25165824 | bytes 12582912 | tf_op jit(solution)/shard_map/concatenate | solution.py:211
  862.7 15.7 %fusion.32 = bf16[1,1024,512]{2,1,0:T(8,128)(2,1)} fusion(bf16[8192,1024]{1,0:T(8,128)(2,1)} %all-gather.7.cloned.1.call-done, bf16[8192,512]{1,0:T(8,128)(2,1)} %get-tuple-element.64), kind=kOutput, calls=%fused_computation.61 | convolution fusion | flops 8590458880 | bytes 26214400 | tf_op jit(solution)/shard_map/rd,rf->df/dot_general | solution.py:145
  878.5 16.1 %fusion.31 = bf16[1,1024,512]{2,1,0:T(8,128)(2,1)} fusion(bf16[8192,1024]{1,0:T(8,128)(2,1)} %all-gather.7.cloned.1.call-done, bf16[8192,512]{1,0:T(8,128)(2,1)} %get-tuple-element.65), kind=kOutput, calls=%fused_computation.60 | convolution fusion | flops 8590458880 | bytes 26214400 | tf_op jit(solution)/shard_map/rd,rf->df/dot_general | solution.py:144
  895.0 18.9 %fusion.38 = bf16[1,512,1024]{2,1,0:T(8,128)(2,1)} fusion(bf16[8192,512]{1,0:T(8,128)(2,1)} %get-tuple-element.66, bf16[8192,1024]{1,0:T(8,128)(2,1)} %all-gather.15.cloned.1.call-done, f32[8192]{0:T(1024)S(1)} %bitcast.186), kind=kOutput, calls=%fused_computation.66 | convolution fusion | flops 8615624704 | bytes 26247168 | tf_op jit(solution)/shard_map/rf,rd->fd/dot_general | solution.py:138
  925.6 51.4 %reduce-scatter.19.cloned.1.call-done = bf16[32,3072]{1,0:T(8,128)(2,1)} async-done(((bf16[1024,3072]{1,0:T(8,128)(2,1)}), bf16[32,3072]{1,0:T(8,128)(2,1)}) %reduce-scatter.19.cloned.1.call-update) | async-done | bytes 196624 | tf_op jit(solution)/shard_map/reduce_scatter | solution.py:212
  976.9 22.2 %reduce-scatter.15.cloned.1.call-done = bf16[1,1024,256]{2,1,0:T(8,128)(2,1)} async-done(((bf16[1,1024,512]{2,1,0:T(8,128)(2,1)}), bf16[1,1024,256]{2,1,0:T(8,128)(2,1)}) %reduce-scatter.15.cloned.1.call-update) | async-done | bytes 524304 | tf_op jit(solution)/shard_map/reduce_scatter | solution.py:155
  1001.2 21.0 %reduce-scatter.13.cloned.1.call-done = bf16[1,1024,256]{2,1,0:T(8,128)(2,1)} async-done(((bf16[1,1024,512]{2,1,0:T(8,128)(2,1)}), bf16[1,1024,256]{2,1,0:T(8,128)(2,1)}) %reduce-scatter.13.cloned.1.call-update) | async-done | bytes 524304 | tf_op jit(solution)/shard_map/reduce_scatter | solution.py:152
  1024.3 21.2 %reduce-scatter.17.cloned.1.call-done = bf16[1,256,1024]{2,1,0:T(8,128)(2,1)} async-done(((bf16[1,512,1024]{2,1,0:T(8,128)(2,1)}), bf16[1,256,1024]{2,1,0:T(8,128)(2,1)}) %reduce-scatter.17.cloned.1.call-update) | async-done | bytes 524304 | tf_op jit(solution)/shard_map/reduce_scatter | solution.py:158
  1051.4 120.4 %all-reduce.2.cloned.1.call-done = f32[144,128]{1,0:T(8,128)} async-done(((f32[144,128]{1,0:T(8,128)}), f32[144,128]{1,0:T(8,128)}) %all-reduce.2.cloned.1.call-update) | async-done | bytes 73744 | tf_op jit(solution)/shard_map/psum | solution.py:214
  1174.9 71.2 %all-gather.17.cloned.1.call-done = bf16[1024,3072]{1,0:T(8,128)(2,1)} async-done(((bf16[32,3072]{1,0:T(8,128)(2,1)}), bf16[1024,3072]{1,0:T(8,128)(2,1)}) %all-gather.17.cloned.1.call-update) | async-done | bytes 6291472 | tf_op jit(solution)/shard_map/all_gather | solution.py:213
  (222 shorter events, 135.5 us)
Async XLA Ops:
  7.2 34.9 %copy-start = (bf16[1024,1024]{1,0:T(8,128)(2,1)S(1)}, bf16[1024,1024]{1,0:T(8,128)(2,1)}, u32[]{:S(2)}) copy-start(bf16[1024,1024]{1,0:T(8,128)(2,1)} %param.21) | copy-start | bytes 6291460
  7.2 51.7 %all-gather.11.cloned.1.call-start = ((), (), s32[]{:S(2)}) async-start(), calls=%async_computation.10 | async-start | bytes 1572864 | tf_op jit(solution)/shard_map/all_gather | solution.py:77
  8.0 167.9 %all-gather.7.cloned.1.call-start = ((), (), s32[]{:S(2)}) async-start(), calls=%async_computation.8 | async-start | bytes 17825792 | tf_op jit(solution)/shard_map/all_gather | solution.py:117
  46.1 150.8 %all-gather.9.cloned.1.call-start = ((), (), s32[]{:S(2)}) async-start(), calls=%async_computation.9 | async-start | bytes 1572864 | tf_op jit(solution)/shard_map/all_gather | solution.py:76
  46.8 172.8 %all-gather.13.cloned.1.call-start = ((), (), s32[]{:S(2)}) async-start(), calls=%async_computation.11 | async-start | bytes 1572864 | tf_op jit(solution)/shard_map/all_gather | solution.py:78
  47.4 300.7 %all-gather.15.cloned.1.call-start = ((), (), s32[]{:S(2)}) async-start(), calls=%async_computation.13 | async-start | bytes 17825792 | tf_op jit(solution)/shard_map/all_gather | solution.py:74
  51.5 161.3 %all-to-all-start = ((f32[16,1,512]{2,1,0:T(1,128)}), f32[16,1,512]{2,1,0:T(1,128)S(1)}, u32[]{:S(2)}, u32[]{:S(2)}) async-start(f32[16,1,512]{2,1,0:T(1,128)} %copy.73), calls=%async_computation | async-start | bytes 65536 | tf_op jit(solution)/shard_map/all_to_all | solution.py:115
  58.9 537.4 %reduce-scatter.11.cloned.1.call-start = ((), (), s32[]{:S(2)}) async-start(), calls=%async_computation.14 | async-start | bytes 17825792 | tf_op jit(solution)/shard_map/reduce_scatter | solution.py:150
  212.8 207.9 %copy-start.50 = (f32[16,1,512]{2,1,0:T(1,128)}, f32[16,1,512]{2,1,0:T(1,128)S(1)}, u32[]{:S(2)}) copy-start(f32[16,1,512]{2,1,0:T(1,128)S(1)} %all-to-all-done) | copy-start | bytes 98308
  348.1 32.2 %copy-start.62 = (bf16[1,1024,512]{2,1,0:T(8,128)(2,1)S(1)}, bf16[1,1024,512]{2,1,0:T(8,128)(2,1)}, u32[]{:S(2)}) copy-start(bf16[1,1024,512]{2,1,0:T(8,128)(2,1)} %all-gather.9.cloned.1.call-done) | copy-start | bytes 3145732
  420.7 356.2 %reduce-scatter.9.cloned.1.call-start = ((), (), s32[]{:S(2)}) async-start(), calls=%async_computation.12 | async-start | bytes 17825792 | tf_op jit(solution)/shard_map/reduce_scatter | solution.py:122
  445.6 150.7 %copy-start.41 = (bf16[1024,16]{0,1:T(8,128)(2,1)S(1)}, bf16[1024,16]{0,1:T(8,128)(2,1)}, u32[]{:S(2)}) copy-start(bf16[1024,16]{0,1:T(8,128)(2,1)} %param.23) | copy-start | bytes 98308
  445.6 150.7 %copy-start.47 = (f32[1024]{0:T(1024)S(1)}, f32[1024]{0:T(1024)}, u32[]{:S(2)}) copy-start(f32[1024]{0:T(1024)} %param.22) | copy-start | bytes 12292
  445.6 150.7 %copy-start.49 = (f32[512]{0:T(512)S(1)}, f32[512]{0:T(512)}, u32[]{:S(2)}) copy-start(f32[512]{0:T(512)} %copy-done.48) | copy-start | bytes 6148
  445.7 331.2 %copy-start.10 = (bf16[512,1024]{1,0:T(8,128)(2,1)S(1)}, bf16[512,1024]{1,0:T(8,128)(2,1)}, u32[]{:S(2)}) copy-start(bf16[512,1024]{1,0:T(8,128)(2,1)} %param.27) | copy-start | bytes 3145732
  445.7 331.2 %copy-start.58 = (f32[512]{0:T(512)S(1)}, f32[512]{0:T(512)}, u32[]{:S(2)}) copy-start(f32[512]{0:T(512)} %get-tuple-element.87) | copy-start | bytes 6148
  445.7 531.2 %reduce-scatter.19.cloned.1.call-start = ((), (), s32[]{:S(2)}) async-start(), calls=%async_computation.20 | async-start | bytes 6488064 | tf_op jit(solution)/shard_map/reduce_scatter | solution.py:212
  455.1 326.0 %copy-start.36 = (f32[16,1,512]{2,1,0:T(1,128)}, f32[16,1,512]{2,1,0:T(1,128)S(1)}, u32[]{:S(2)}) copy-start(f32[16,1,512]{2,1,0:T(1,128)S(1)} %all_to_all.21) | copy-start | bytes 98308
  862.7 136.5 %reduce-scatter.15.cloned.1.call-start = ((), (), s32[]{:S(2)}) async-start(), calls=%async_computation.18 | async-start | bytes 1572864 | tf_op jit(solution)/shard_map/reduce_scatter | solution.py:155
  878.5 143.7 %reduce-scatter.13.cloned.1.call-start = ((), (), s32[]{:S(2)}) async-start(), calls=%async_computation.17 | async-start | bytes 1572864 | tf_op jit(solution)/shard_map/reduce_scatter | solution.py:152
  894.7 150.8 %reduce-scatter.17.cloned.1.call-start = ((), (), s32[]{:S(2)}) async-start(), calls=%async_computation.19 | async-start | bytes 1572864 | tf_op jit(solution)/shard_map/reduce_scatter | solution.py:158
  913.9 257.9 %all-reduce.2.cloned.1.call-start = ((), (), s32[]{:S(2)}) async-start(), calls=%async_computation.15 | async-start | bytes 147456 | tf_op jit(solution)/shard_map/psum | solution.py:214
  924.6 123.0 %copy-start.57 = (f32[512]{0:T(512)S(1)}, f32[512]{0:T(512)}, u32[]{:S(2)}) copy-start(f32[512]{0:T(512)} %get-tuple-element.85) | copy-start | bytes 6148
  925.3 320.8 %all-gather.17.cloned.1.call-start = ((), (), s32[]{:S(2)}) async-start(), calls=%async_computation.16 | async-start | bytes 6488064 | tf_op jit(solution)/shard_map/all_gather | solution.py:213
  (57 other events, 405.5 us)
Sparse Core Ops, SparseCore 0:
  9.6 23.9 all-gather.10
  46.2 129.6 all-gather.6
  177.4 19.4 all-gather.8
  198.3 21.2 all-gather.12
  221.6 126.4 all-gather.14
  420.8 175.4 reduce-scatter.10
  600.4 176.4 reduce-scatter.8
  862.8 114.0 reduce-scatter.18
  979.7 19.3 reduce-scatter.14
  1001.8 20.3 reduce-scatter.12
  1025.0 20.3 reduce-scatter.16
  1051.5 120.2 all-reduce.1
  1174.7 71.3 all-gather.16
where the time goes:
time: 1270 us; the launch traced here: 1260 us
  waiting for transfers between devices  884 us (70%)
  matrix products  258 us (20%)
  other arithmetic  56.7 us (4%)
  local copies, waits for them, and re-layouts  30 us (2%)
  between operations  15.1 us (1%)
    reduce_scatter x1, waiting for transfers between devices, on_device(): lax.psum_scatter((row_gates * outputs.astype(f32)).astype(bf16), 'wide',...  177 us
    reduce_scatter x1, waiting for transfers between devices, on_device(): lax.psum_scatter(copy_grads, 'wide', scatter_dimension=0, tiled=True)  141 us
    all_gather x1, waiting for transfers between devices, on_device(): rows_grad = lax.all_gather(grad_out, 'wide', axis=0, tiled=True)  128 us
    psum x1, waiting for transfers between devices, on_device(): small = lax.psum(small, everywhere)  120 us
    all_gather x1, waiting for transfers between devices, on_device(): rows_in = lax.all_gather(ffn_normed, 'wide', axis=0, tiled=True)  117 us
    all_gather x1, waiting for transfers between devices, on_device(): columns = lax.all_gather(shares, everywhere, axis=0, tiled=True).astype(f32)  71.2 us
    reduce_scatter x1, waiting for transfers between devices, on_device(): lax.psum_scatter(columns.astype(bf16), everywhere, scatter_dimension=0, t...  51.4 us
    dot_general x1, matrix products, on_device(): jnp.einsum('rd,fd->rf', grads_in, full_down[0], preferred_element_type=f32)  32.2 us
  transfers between devices with their start and end apart: 14, of which 12 were waited for; matrix products, arithmetic and copies ran while one was open for 14% of the time, Pallas kernels for 0%

commit v1 on v0

--- a/solution.py
+++ b/solution.py
@@ -5,6 +5,12 @@
 
 HD = 64
 EPSILON = 1e-05
+
+
+def summed_here(x, mesh_axis):
+    parts = lax.all_gather(x, mesh_axis, axis=0, tiled=False)
+    total = parts.sum(axis=0)
+    return total
 
 
 def norm_scale(values):
@@ -211,7 +217,7 @@
     columns = jnp.concatenate([query_w_grad, key_w_grad, value_w_grad, out_w_grad], axis=1)
     shares = lax.psum_scatter(columns.astype(bf16), everywhere, scatter_dimension=0, tiled=True)
     columns = lax.all_gather(shares, everywhere, axis=0, tiled=True).astype(f32)
-    small = lax.psum(small, everywhere)
+    small = summed_here(small, everywhere)
     gain_rows = model_width // 128
     query_width, key_width = (w_query.shape[1], w_key.shape[1])
     summed = (

time: 1270 us -> 1200 us (0.945)
  waiting for transfers between devices: 884 us -> 815 us
    psum x1 -> x0, waiting for transfers between devices: 120 us -> none  [on_device(): small = lax.psum(small, everywhere)]
    all_gather x0 -> x1, waiting for transfers between devices: none -> 54.6 us  [summed_here(): parts = lax.all_gather(x, mesh_axis, axis=0, tiled=False)]
  transfers between devices with their start and end apart: 14 -> 14, of which waited for: 12 -> 12; matrix products, arithmetic and copies ran while one was open for 14% -> 15% of each run, Pallas kernels for 0% -> 0%
where the time goes in v1:
time: 1200 us; the launch traced here: 1190 us
  waiting for transfers between devices  815 us (68%)
  matrix products  258 us (22%)
  other arithmetic  58.5 us (5%)
  local copies, waits for them, and re-layouts  28.5 us (2%)
  between operations  15.1 us (1%)
    reduce_scatter x1, waiting for transfers between devices, on_device(): lax.psum_scatter((row_gates * outputs.astype(f32)).astype(bf16), 'wide',...  177 us
    reduce_scatter x1, waiting for transfers between devices, on_device(): lax.psum_scatter(copy_grads, 'wide', scatter_dimension=0, tiled=True)  141 us
    all_gather x1, waiting for transfers between devices, on_device(): rows_grad = lax.all_gather(grad_out, 'wide', axis=0, tiled=True)  128 us
    all_gather x1, waiting for transfers between devices, on_device(): rows_in = lax.all_gather(ffn_normed, 'wide', axis=0, tiled=True)  117 us
    all_gather x1, waiting for transfers between devices, on_device(): columns = lax.all_gather(shares, everywhere, axis=0, tiled=True).astype(f32)  67.6 us
    all_gather x1, waiting for transfers between devices, summed_here(): parts = lax.all_gather(x, mesh_axis, axis=0, tiled=False)  54.6 us
    reduce_scatter x1, waiting for transfers between devices, on_device(): lax.psum_scatter(columns.astype(bf16), everywhere, scatter_dimension=0, t...  51.4 us
    dot_general x1, matrix products, on_device(): jnp.einsum('rd,fd->rf', grads_in, full_down[0], preferred_element_type=f32)  32.2 us
  transfers between devices with their start and end apart: 14, of which 12 were waited for; matrix products, arithmetic and copies ran while one was open for 15% of the time, Pallas kernels for 0%

profile of v1, /device:TPU:0, one launch (start us, length us, event | category | flops | bytes accessed | tf_op | source)
XLA Modules:
  0.0 1192.5 jit_solution(17818200200947158228)
XLA Ops:
  58.9 116.9 %all-gather.9.cloned.1.call-done = bf16[8192,1024]{1,0:T(8,128)(2,1)} async-done(((bf16[512,1024]{1,0:T(8,128)(2,1)}), bf16[8192,1024]{1,0:T(8,128)(2,1)}) %all-gather.9.cloned.1.call-update) | async-done | bytes 16777232 | tf_op jit(solution)/shard_map/all_gather | solution.py:123
  175.9 16.5 %fusion.47 = f32[8192,512]{1,0:T(8,128)} fusion(bf16[8192,1024]{1,0:T(8,128)(2,1)} %all-gather.9.cloned.1.call-done, bf16[1,1024,512]{2,1,0:T(8,128)(2,1)} %all-gather.13.cloned.1.call-done), kind=kOutput, calls=%fused_computation.74 | convolution fusion | flops 8589934592 | bytes 34603008 | tf_op jit(solution)/shard_map/dot_general | solution.py:125
  196.9 16.0 %fusion.51 = f32[8192,512]{1,0:T(8,128)} fusion(bf16[8192,1024]{1,0:T(8,128)(2,1)} %all-gather.9.cloned.1.call-done, bf16[1,1024,512]{2,1,0:T(8,128)(2,1)} %all-gather.11.cloned.1.call-done), kind=kOutput, calls=%fused_computation.78 | convolution fusion | flops 8589934592 | bytes 34603008 | tf_op jit(solution)/shard_map/dot_general | solution.py:124
  219.6 128.5 %all-gather.17.cloned.1.call-done = bf16[8192,1024]{1,0:T(8,128)(2,1)} async-done(((bf16[512,1024]{1,0:T(8,128)(2,1)}), bf16[8192,1024]{1,0:T(8,128)(2,1)}) %all-gather.17.cloned.1.call-update) | async-done | bytes 16777232 | tf_op jit(solution)/shard_map/all_gather | solution.py:80
  348.1 32.2 %multiply_convert_fusion = (bf16[8192,512]{1,0:T(8,128)(2,1)}, bf16[8192,512]{1,0:T(8,128)(2,1)}, bf16[8192,512]{1,0:T(8,128)(2,1)}) fusion(f32[8192,512]{1,0:T(8,128)} %fusion.51, f32[8192,512]{1,0:T(8,128)} %fusion.47, bf16[1,512,1024]{2,1,0:T(8,128)(2,1)} %all-gather.15.cloned.1.call-done, bf16[8192,1024]{1,0:T(8,128)(2,1)} %all-gather.17.cloned.1.call-done, ...), kind=kOutput, calls=%fused_computation.13 | convolution fusion | flops 8682209280 | bytes 76578816 | tf_op jit(solution)/shard_map/rd,fd->rf/dot_general | solution.py:143
  380.3 18.8 %fusion.49 = f32[8192,1024]{1,0:T(8,128)} fusion(bf16[8192,512]{1,0:T(8,128)(2,1)} %get-tuple-element.65, bf16[1,1024,512]{2,1,0:T(8,128)(2,1)S(1)} %copy-done.62), kind=kOutput, calls=%fused_computation.76 | convolution fusion | flops 8589934592 | bytes 42991616 | tf_op jit(solution)/shard_map/rf,df->rd/dot_general | solution.py:153
  399.1 21.5 %add_convert_fusion = bf16[8192,1024]{1,0:T(8,128)(2,1)} fusion(f32[8192,1024]{1,0:T(8,128)} %fusion.49, bf16[8192,512]{1,0:T(8,128)(2,1)} %get-tuple-element.64, bf16[1,1024,512]{2,1,0:T(8,128)(2,1)S(1)} %copy-done.60), kind=kOutput, calls=%fused_computation.6 | convolution fusion | flops 8606711808 | bytes 59768832 | tf_op jit(solution)/shard_map/rf,df->rd/dot_general | solution.py:154
  421.9 23.7 %fusion.1 = (f32[8192]{0:T(1024)S(1)}, bf16[8192,1024]{1,0:T(8,128)(2,1)}) fusion(bf16[8192,1024]{1,0:T(8,128)(2,1)} %all-gather.17.cloned.1.call-done, f32[8192]{0:T(1024)S(1)} %bitcast.187, bf16[8192,512]{1,0:T(8,128)(2,1)} %get-tuple-element.66, bf16[1,512,1024]{2,1,0:T(8,128)(2,1)S(1)} %copy-done.61), kind=kOutput, calls=%fused_computation.4 | convolution fusion | flops 8648646656 | bytes 43057152 | tf_op jit(solution)/shard_map/dot_general | solution.py:127
  445.7 9.3 all_to_all.21
  455.1 141.1 %reduce-scatter.11.cloned.1.call-done = bf16[512,1024]{1,0:T(8,128)(2,1)} async-done(((bf16[8192,1024]{1,0:T(8,128)(2,1)}), bf16[512,1024]{1,0:T(8,128)(2,1)}) %reduce-scatter.11.cloned.1.call-update) | async-done | bytes 1048592 | tf_op jit(solution)/shard_map/reduce_scatter | solution.py:156
  600.2 176.6 %reduce-scatter.9.cloned.1.call-done = bf16[512,1024]{1,0:T(8,128)(2,1)} async-done(((bf16[8192,1024]{1,0:T(8,128)(2,1)}), bf16[512,1024]{1,0:T(8,128)(2,1)}) %reduce-scatter.9.cloned.1.call-update) | async-done | bytes 1048592 | tf_op jit(solution)/shard_map/reduce_scatter | solution.py:128
  788.5 9.4 fusion.41
  797.9 16.0 %fusion.3 = (f32[8,2,512]{2,1,0:T(2,128)}, f32[8,512,512,2]{2,1,3,0:T(8,128)}) fusion(f32[8,2,512,512]{2,3,1,0:T(8,128)} %get-tuple-element.93, f32[8,2,512]{2,1,0:T(2,128)S(1)} %bitcast.183, bf16[512,8,64,1]{0,2,3,1:T(8,128)(2,1)} %bitcast.167, bf16[512,8,2,64]{0,3,2,1:T(8,128)(2,1)} %bitcast.161), kind=kOutput, calls=%fused_computation.9 | convolution fusion | flops 549445632 | bytes 35192832 | tf_op jit(solution)/shard_map/qngd,knd->ngqk/dot_general | solution.py:182
  814.0 11.1 fusion.5
  838.8 15.2 %pad_maximum_fusion = bf16[1024,3072]{0,1:T(8,128)(2,1)} fusion(bf16[1024,1024]{0,1:T(8,128)(2,1)S(1)} %copy-done.20, bf16[1024,512]{0,1:T(8,128)(2,1)S(1)} %convolution_convert_fusion.6, bf16[1024,512]{0,1:T(8,128)(2,1)S(1)} %convolution_convert_fusion.7, bf16[1024,1024]{0,1:T(8,128)(2,1)S(1)} %convolution_convert_fusion.1), kind=kLoop, calls=%fused_computation.23 | loop fusion | flops 25165824 | bytes 12582912 | tf_op jit(solution)/shard_map/concatenate | solution.py:217
  862.7 15.7 %fusion.32 = bf16[1,1024,512]{2,1,0:T(8,128)(2,1)} fusion(bf16[8192,1024]{1,0:T(8,128)(2,1)} %all-gather.9.cloned.1.call-done, bf16[8192,512]{1,0:T(8,128)(2,1)} %get-tuple-element.64), kind=kOutput, calls=%fused_computation.61 | convolution fusion | flops 8590458880 | bytes 26214400 | tf_op jit(solution)/shard_map/rd,rf->df/dot_general | solution.py:151
  878.5 16.1 %fusion.31 = bf16[1,1024,512]{2,1,0:T(8,128)(2,1)} fusion(bf16[8192,1024]{1,0:T(8,128)(2,1)} %all-gather.9.cloned.1.call-done, bf16[8192,512]{1,0:T(8,128)(2,1)} %get-tuple-element.65), kind=kOutput, calls=%fused_computation.60 | convolution fusion | flops 8590458880 | bytes 26214400 | tf_op jit(solution)/shard_map/rd,rf->df/dot_general | solution.py:150
  895.0 18.9 %fusion.38 = bf16[1,512,1024]{2,1,0:T(8,128)(2,1)} fusion(bf16[8192,512]{1,0:T(8,128)(2,1)} %get-tuple-element.66, bf16[8192,1024]{1,0:T(8,128)(2,1)} %all-gather.17.cloned.1.call-done, f32[8192]{0:T(1024)S(1)} %bitcast.188), kind=kOutput, calls=%fused_computation.66 | convolution fusion | flops 8615624704 | bytes 26247168 | tf_op jit(solution)/shard_map/rf,rd->fd/dot_general | solution.py:144
  925.6 51.4 %reduce-scatter.19.cloned.1.call-done = bf16[32,3072]{1,0:T(8,128)(2,1)} async-done(((bf16[1024,3072]{1,0:T(8,128)(2,1)}), bf16[32,3072]{1,0:T(8,128)(2,1)}) %reduce-scatter.19.cloned.1.call-update) | async-done | bytes 196624 | tf_op jit(solution)/shard_map/reduce_scatter | solution.py:218
  976.9 22.2 %reduce-scatter.15.cloned.1.call-done = bf16[1,1024,256]{2,1,0:T(8,128)(2,1)} async-done(((bf16[1,1024,512]{2,1,0:T(8,128)(2,1)}), bf16[1,1024,256]{2,1,0:T(8,128)(2,1)}) %reduce-scatter.15.cloned.1.call-update) | async-done | bytes 524304 | tf_op jit(solution)/shard_map/reduce_scatter | solution.py:161
  1001.2 21.0 %reduce-scatter.13.cloned.1.call-done = bf16[1,1024,256]{2,1,0:T(8,128)(2,1)} async-done(((bf16[1,1024,512]{2,1,0:T(8,128)(2,1)}), bf16[1,1024,256]{2,1,0:T(8,128)(2,1)}) %reduce-scatter.13.cloned.1.call-update) | async-done | bytes 524304 | tf_op jit(solution)/shard_map/reduce_scatter | solution.py:158
  1024.3 21.2 %reduce-scatter.17.cloned.1.call-done = bf16[1,256,1024]{2,1,0:T(8,128)(2,1)} async-done(((bf16[1,512,1024]{2,1,0:T(8,128)(2,1)}), bf16[1,256,1024]{2,1,0:T(8,128)(2,1)}) %reduce-scatter.17.cloned.1.call-update) | async-done | bytes 524304 | tf_op jit(solution)/shard_map/reduce_scatter | solution.py:164
  1051.4 54.6 %all-gather.21.cloned.1.call-done = f32[4608,128]{1,0:T(8,128)} async-done(((f32[144,128]{1,0:T(8,128)}), f32[4608,128]{1,0:T(8,128)}) %all-gather.21.cloned.1.call-update) | async-done | bytes 2359312 | tf_op jit(solution)/shard_map/all_gather | solution.py:11
  1109.3 67.6 %all-gather.19.cloned.1.call-done = bf16[1024,3072]{1,0:T(8,128)(2,1)} async-done(((bf16[32,3072]{1,0:T(8,128)(2,1)}), bf16[1024,3072]{1,0:T(8,128)(2,1)}) %all-gather.19.cloned.1.call-update) | async-done | bytes 6291472 | tf_op jit(solution)/shard_map/all_gather | solution.py:219
  (223 shorter events, 135.8 us)
Async XLA Ops:
  7.2 34.9 %copy-start = (bf16[1024,1024]{1,0:T(8,128)(2,1)S(1)}, bf16[1024,1024]{1,0:T(8,128)(2,1)}, u32[]{:S(2)}) copy-start(bf16[1024,1024]{1,0:T(8,128)(2,1)} %param.21) | copy-start | bytes 6291460
  7.2 51.7 %all-gather.13.cloned.1.call-start = ((), (), s32[]{:S(2)}) async-start(), calls=%async_computation.10 | async-start | bytes 1572864 | tf_op jit(solution)/shard_map/all_gather | solution.py:83
  8.0 167.9 %all-gather.9.cloned.1.call-start = ((), (), s32[]{:S(2)}) async-start(), calls=%async_computation.8 | async-start | bytes 17825792 | tf_op jit(solution)/shard_map/all_gather | solution.py:123
  46.1 150.8 %all-gather.11.cloned.1.call-start = ((), (), s32[]{:S(2)}) async-start(), calls=%async_computation.9 | async-start | bytes 1572864 | tf_op jit(solution)/shard_map/all_gather | solution.py:82
  46.8 172.8 %all-gather.15.cloned.1.call-start = ((), (), s32[]{:S(2)}) async-start(), calls=%async_computation.11 | async-start | bytes 1572864 | tf_op jit(solution)/shard_map/all_gather | solution.py:84
  47.4 300.7 %all-gather.17.cloned.1.call-start = ((), (), s32[]{:S(2)}) async-start(), calls=%async_computation.13 | async-start | bytes 17825792 | tf_op jit(solution)/shard_map/all_gather | solution.py:80
  51.5 161.3 %all-to-all-start = ((f32[16,1,512]{2,1,0:T(1,128)}), f32[16,1,512]{2,1,0:T(1,128)S(1)}, u32[]{:S(2)}, u32[]{:S(2)}) async-start(f32[16,1,512]{2,1,0:T(1,128)} %copy.73), calls=%async_computation | async-start | bytes 65536 | tf_op jit(solution)/shard_map/all_to_all | solution.py:121
  58.9 537.4 %reduce-scatter.11.cloned.1.call-start = ((), (), s32[]{:S(2)}) async-start(), calls=%async_computation.14 | async-start | bytes 17825792 | tf_op jit(solution)/shard_map/reduce_scatter | solution.py:156
  212.8 207.9 %copy-start.50 = (f32[16,1,512]{2,1,0:T(1,128)}, f32[16,1,512]{2,1,0:T(1,128)S(1)}, u32[]{:S(2)}) copy-start(f32[16,1,512]{2,1,0:T(1,128)S(1)} %all-to-all-done) | copy-start | bytes 98308
  348.1 32.2 %copy-start.62 = (bf16[1,1024,512]{2,1,0:T(8,128)(2,1)S(1)}, bf16[1,1024,512]{2,1,0:T(8,128)(2,1)}, u32[]{:S(2)}) copy-start(bf16[1,1024,512]{2,1,0:T(8,128)(2,1)} %all-gather.11.cloned.1.call-done) | copy-start | bytes 3145732
  420.7 356.2 %reduce-scatter.9.cloned.1.call-start = ((), (), s32[]{:S(2)}) async-start(), calls=%async_computation.12 | async-start | bytes 17825792 | tf_op jit(solution)/shard_map/reduce_scatter | solution.py:128
  445.6 150.7 %copy-start.41 = (bf16[1024,16]{0,1:T(8,128)(2,1)S(1)}, bf16[1024,16]{0,1:T(8,128)(2,1)}, u32[]{:S(2)}) copy-start(bf16[1024,16]{0,1:T(8,128)(2,1)} %param.23) | copy-start | bytes 98308
  445.6 150.7 %copy-start.47 = (f32[1024]{0:T(1024)S(1)}, f32[1024]{0:T(1024)}, u32[]{:S(2)}) copy-start(f32[1024]{0:T(1024)} %param.22) | copy-start | bytes 12292
  445.6 150.7 %copy-start.49 = (f32[512]{0:T(512)S(1)}, f32[512]{0:T(512)}, u32[]{:S(2)}) copy-start(f32[512]{0:T(512)} %copy-done.48) | copy-start | bytes 6148
  445.7 331.2 %copy-start.10 = (bf16[512,1024]{1,0:T(8,128)(2,1)S(1)}, bf16[512,1024]{1,0:T(8,128)(2,1)}, u32[]{:S(2)}) copy-start(bf16[512,1024]{1,0:T(8,128)(2,1)} %param.27) | copy-start | bytes 3145732
  445.7 331.2 %copy-start.58 = (f32[512]{0:T(512)S(1)}, f32[512]{0:T(512)}, u32[]{:S(2)}) copy-start(f32[512]{0:T(512)} %get-tuple-element.87) | copy-start | bytes 6148
  445.7 531.2 %reduce-scatter.19.cloned.1.call-start = ((), (), s32[]{:S(2)}) async-start(), calls=%async_computation.20 | async-start | bytes 6488064 | tf_op jit(solution)/shard_map/reduce_scatter | solution.py:218
  455.1 326.0 %copy-start.36 = (f32[16,1,512]{2,1,0:T(1,128)}, f32[16,1,512]{2,1,0:T(1,128)S(1)}, u32[]{:S(2)}) copy-start(f32[16,1,512]{2,1,0:T(1,128)S(1)} %all_to_all.21) | copy-start | bytes 98308
  862.7 136.5 %reduce-scatter.15.cloned.1.call-start = ((), (), s32[]{:S(2)}) async-start(), calls=%async_computation.17 | async-start | bytes 1572864 | tf_op jit(solution)/shard_map/reduce_scatter | solution.py:161
  878.5 143.7 %reduce-scatter.13.cloned.1.call-start = ((), (), s32[]{:S(2)}) async-start(), calls=%async_computation.16 | async-start | bytes 1572864 | tf_op jit(solution)/shard_map/reduce_scatter | solution.py:158
  894.7 150.8 %reduce-scatter.17.cloned.1.call-start = ((), (), s32[]{:S(2)}) async-start(), calls=%async_computation.18 | async-start | bytes 1572864 | tf_op jit(solution)/shard_map/reduce_scatter | solution.py:164
  913.9 192.1 %all-gather.21.cloned.1.call-start = ((), (), s32[]{:S(2)}) async-start(), calls=%async_computation.19 | async-start | bytes 2433024 | tf_op jit(solution)/shard_map/all_gather | solution.py:11
  924.6 123.0 %copy-start.57 = (f32[512]{0:T(512)S(1)}, f32[512]{0:T(512)}, u32[]{:S(2)}) copy-start(f32[512]{0:T(512)} %get-tuple-element.85) | copy-start | bytes 6148
  925.3 251.7 %all-gather.19.cloned.1.call-start = ((), (), s32[]{:S(2)}) async-start(), calls=%async_computation.15 | async-start | bytes 6488064 | tf_op jit(solution)/shard_map/all_gather | solution.py:219
  (57 other events, 405.5 us)
Sparse Core Ops, SparseCore 0:
  9.6 23.9 all-gather.12
  46.2 129.6 all-gather.8
  177.4 19.4 all-gather.10
  198.3 21.2 all-gather.14
  221.6 126.4 all-gather.16
  420.8 175.4 reduce-scatter.10
  600.4 176.4 reduce-scatter.8
  862.8 114.0 reduce-scatter.18
  979.7 19.3 reduce-scatter.14
  1001.8 20.3 reduce-scatter.12
  1025.0 20.3 reduce-scatter.16
  1048.8 57.0 all-gather.20
  1108.8 68.0 all-gather.18
